TPU v7x, 32 devices: a whole 2x2x4 slice. The times are simulated.
32 devices in a mesh: row: 2 (over x), col: 16 (over z, y, core).
Axes of the slice: x: 2, y: 2, z: 4, core: 2. Of those that a mesh axis runs over, the one named last changes fastest.
Arguments:
- ld_matrix: bfloat16 [32768, 32768], P('row', 'col'), may hold values from -0.23925781 to 0.23925781
- factor: float32 [32768, 256], P(('row', 'col')), may hold values from -0.24 to 0.24
- diag_values: bfloat16 [32768], P('col'), may hold values from 0.5 to 4
Outputs:
- factor_grad: float32 [32768, 256], P(('row', 'col'))
All inputs are finite; a program needn't handle non-finite values.
Results may differ from a plain program's by a relative error of at most 0.003.
Values may be sent and summed in bfloat16 or wider, within the bound.
A program may use at most 128 MiB of HBM per device.

v0:
```python
import math
import jax
import jax.numpy as jnp
from jax import lax
from jax.sharding import PartitionSpec as P


def from_root(value, axis, source):
    kept = jnp.where(lax.axis_index(axis) == source, value, 0).astype(value.dtype)
    return lax.psum(kept, axis)


def local(ld_matrix, factor, diag_values):
    factor_low = factor.astype(jnp.bfloat16)
    row_height = ld_matrix.shape[0]
    col_width = ld_matrix.shape[1]
    rank_width = factor.shape[1]
    row_panel = lax.all_gather(factor_low, "col", axis=0, tiled=True)
    col_index = lax.axis_index("col")
    row_index = lax.axis_index("row")
    per_row = lax.axis_size("col") // lax.axis_size("row")
    offset = col_index % per_row * col_width
    section = lax.dynamic_slice_in_dim(row_panel, offset, col_width, 0)
    col_panel = from_root(section, "row", col_index // per_row)
    diag_float = diag_values.astype(jnp.float32)
    col_ids = col_index * col_width + jnp.arange(col_width, dtype=jnp.int32)
    own_rows = row_height // lax.axis_size("col")
    height = math.gcd(own_rows * lax.axis_size("col"), 512)
    number = own_rows * lax.axis_size("col") // height

    def one_block(number_index):
        first = number_index * height
        ld_block = lax.dynamic_slice_in_dim(ld_matrix, first, height, 0)
        left = lax.dynamic_slice_in_dim(row_panel, first, height, 0)
        row_ids = row_index * row_height + first + jnp.arange(height, dtype=jnp.int32)
        model_part = jnp.dot(left, col_panel.T, preferred_element_type=jnp.float32)
        ondiag = row_ids[:, None] == col_ids[None, :]
        extra = jnp.where(ondiag, diag_float[None, :], jnp.float32(0.0))
        misfit = (model_part + extra - ld_block.astype(jnp.float32)).astype(jnp.bfloat16)
        return 4.0 * jnp.dot(misfit, col_panel, preferred_element_type=jnp.float32)

    blocks = lax.map(one_block, jnp.arange(number, dtype=jnp.int32))
    return lax.psum_scatter(
        blocks.reshape(own_rows * lax.axis_size("col"), rank_width),
        "col",
        scatter_dimension=0,
        tiled=True,
    )


def solution(mesh):
    in_specs = (P("row", "col"), P(("row", "col"), None), P("col"))
    out_specs = P(("row", "col"), None)
    return jax.shard_map(local, mesh=mesh, in_specs=in_specs, out_specs=out_specs, check_vma=False)
```

profile of v0, /device:TPU:0, one launch (start us, length us, event | category | flops | bytes accessed | tf_op | source)
XLA Modules:
  0.0 495.8 jit_solution(5465250970531595996)
XLA Ops:
  6.5 2.1 convert_element_type.18
  8.7 77.8 %all-gather.2.cloned.1.call-done = bf16[16384,256]{1,0:T(8,128)(2,1)} async-done(((bf16[1024,256]{1,0:T(8,128)(2,1)}), bf16[16384,256]{1,0:T(8,128)(2,1)}) %all-gather.2.cloned.1.call-update) | async-done | bytes 8388624 | tf_op jit(solution)/shard_map/all_gather | solution.py:18
  86.5 2.4 dynamic-slice_select_fusion
  89.0 0.7 convert_element_type.19
  89.7 38.1 %all-reduce.2.cloned.1.call-done = bf16[2048,256]{1,0:T(8,128)(2,1)} async-done(((bf16[2048,256]{1,0:T(8,128)(2,1)}), bf16[2048,256]{1,0:T(8,128)(2,1)}) %all-reduce.2.cloned.1.call-update) | async-done | bytes 1048592 | tf_op jit(solution)/shard_map/psum | solution.py:10
  127.8 183.9 %while.13 = (s32[]{:T(128)}, f32[32,512,256]{2,1,0:T(8,128)}, s32[32]{0:T(128)S(1)}, bf16[16384,256]{1,0:T(8,128)(2,1)}, bf16[2048,256]{1,0:T(8,128)(2,1)}, /*in...) while((s32[]{:T(128)}, f32[32,512,256]{2,1,0:T(8,128)}, ...), condition=%wide.region_2.3_spmd.clone, body=%wide.region_1.2_spmd.clone.sunk | while | flops 1080166912 | bytes 5011147 | solution.py:42
  127.8 0.6 dynamic_slice.35
  129.1 4.5 fusion.18
  133.5 0.6 dynamic_slice.35
  134.8 4.5 fusion.18
  140.6 4.5 fusion.18
  146.3 4.4 fusion.18
  152.0 4.5 fusion.18
  157.7 4.5 fusion.18
  162.2 0.6 dynamic_slice.35
  163.5 4.4 fusion.18
  167.9 0.6 dynamic_slice.35
  169.2 4.6 fusion.18
  175.0 4.5 fusion.18
  179.5 0.6 dynamic_slice.35
  180.8 4.5 fusion.18
  186.6 4.5 fusion.18
  191.1 0.6 dynamic_slice.35
  192.3 4.5 fusion.18
  198.1 4.5 fusion.18
  203.8 4.5 fusion.18
  209.5 4.5 fusion.18
  214.0 0.6 dynamic_slice.35
  215.3 4.6 fusion.18
  221.2 4.6 fusion.18
  227.0 4.5 fusion.18
  231.5 0.6 dynamic_slice.35
  232.8 4.4 fusion.18
  238.5 4.5 fusion.18
  244.2 4.5 fusion.18
  249.9 4.5 fusion.18
  255.7 4.4 fusion.18
  261.4 4.4 fusion.18
  267.1 4.5 fusion.18
  272.9 4.5 fusion.18
  277.4 0.6 dynamic_slice.35
  278.6 4.4 fusion.18
  284.3 4.4 fusion.18
  290.1 4.5 fusion.18
  295.8 4.5 fusion.18
  301.5 4.5 fusion.18
  307.3 4.5 fusion.18
  311.8 177.5 %reduce-scatter.2.cloned.1.call-done = f32[1024,256]{1,0:T(8,128)} async-done(((f32[16384,256]{1,0:T(8,128)}), f32[1024,256]{1,0:T(8,128)}) %reduce-scatter.2.cloned.1.call-update) | async-done | bytes 1048592 | tf_op jit(solution)/shard_map/reduce_scatter | solution.py:43
  (95 shorter events, 13.9 us)
Async XLA Ops:
  6.5 80.0 %all-gather.2.cloned.1.call-start = ((), (), s32[]{:S(2)}) async-start(), calls=%async_computation.1 | async-start | bytes 8912896 | tf_op jit(solution)/shard_map/all_gather | solution.py:18
  8.6 119.2 %all-reduce.2.cloned.1.call-start = ((), (), s32[]{:S(2)}) async-start(), calls=%async_computation.2 | async-start | bytes 2097152 | tf_op jit(solution)/shard_map/psum | solution.py:10
  88.9 400.3 %reduce-scatter.2.cloned.1.call-start = ((), (), s32[]{:S(2)}) async-start(), calls=%async_computation.3 | async-start | bytes 17825792 | tf_op jit(solution)/shard_map/reduce_scatter | solution.py:43
Sparse Core Ops, SparseCore 0:
  9.5 77.0 all-gather.1
  89.1 38.6 all-reduce.1
  311.9 177.3 reduce-scatter.1
where the time goes:
time: 496 us
  waiting for transfers between devices  293 us (59%)
  matrix products  143 us (29%)
  loops' own time  21.6 us (4%)
  local copies, waits for them, and re-layouts  18.6 us (4%)
  between operations  13.1 us (3%)
  other arithmetic  5.51 us (1%)
    reduce_scatter x1, waiting for transfers between devices, local(): lax.psum_scatter(blocks.reshape(own_rows * lax.axis_size('col'), rank_wid...  178 us
    dot_general x32, matrix products, one_block(): return 4.0 * jnp.dot(misfit, col_panel, preferred_element_type=jnp.float32)  143 us
    all_gather x1, waiting for transfers between devices, local(): row_panel = lax.all_gather(factor_low, 'col', axis=0, tiled=True)  77.8 us
    psum x1, waiting for transfers between devices, from_root(): return lax.psum(kept, axis)  38.1 us
    another operation x1, loops' own time, local(): blocks = lax.map(one_block, jnp.arange(number, dtype=jnp.int32))  21.6 us
    dynamic_slice x32, local copies, waits for them, and re-layouts, local(): blocks = lax.map(one_block, jnp.arange(number, dtype=jnp.int32))  18.6 us
  transfers between devices with their start and end apart: 3, of which 3 were waited for; matrix products, arithmetic and copies ran while one was open for 0% of the time, Pallas kernels for 0%

commit v1 on v0

--- a/solution.py
+++ b/solution.py
@@ -4,10 +4,12 @@
 from jax import lax
 from jax.sharding import PartitionSpec as P
 
+reach_rails = lambda mine_x, along_axis: jnp.sum(lax.all_gather(mine_x, along_axis), axis=0)
+
 
 def from_root(value, axis, source):
     kept = jnp.where(lax.axis_index(axis) == source, value, 0).astype(value.dtype)
-    return lax.psum(kept, axis)
+    return reach_rails(kept, axis)
 
 
 def local(ld_matrix, factor, diag_values):

time: 496 us -> 475 us (0.958)
  matrix products: 143 us -> 125 us
  waiting for transfers between devices: 293 us -> 286 us
    psum x1 -> x0, waiting for transfers between devices: 38.1 us -> none  [from_root(): return lax.psum(kept, axis)]
    all_gather x0 -> x1, waiting for transfers between devices: none -> 31.1 us  [lax.all_gather(mine_x, along_axis)]
    dot_general x32, matrix products: 143 us -> 125 us  [one_block(): return 4.0 * jnp.dot(misfit, col_panel, preferred_element_type=jnp.float32)]
where the time goes in v1:
time: 475 us; the launch traced here: 473 us
  waiting for transfers between devices  286 us (60%)
  matrix products  125 us (26%)
  loops' own time  21.6 us (5%)
  local copies, waits for them, and re-layouts  18.6 us (4%)
  between operations  13.2 us (3%)
  other arithmetic  8.15 us (2%)
    reduce_scatter x1, waiting for transfers between devices, local(): lax.psum_scatter(blocks.reshape(own_rows * lax.axis_size('col'), rank_wid...  178 us
    dot_general x32, matrix products, one_block(): return 4.0 * jnp.dot(misfit, col_panel, preferred_element_type=jnp.float32)  125 us
    all_gather x1, waiting for transfers between devices, local(): row_panel = lax.all_gather(factor_low, 'col', axis=0, tiled=True)  77.8 us
    all_gather x1, waiting for transfers between devices, lax.all_gather(mine_x, along_axis)  31.1 us
    another operation x1, loops' own time, local(): blocks = lax.map(one_block, jnp.arange(number, dtype=jnp.int32))  21.6 us
    dynamic_slice x32, local copies, waits for them, and re-layouts, local(): blocks = lax.map(one_block, jnp.arange(number, dtype=jnp.int32))  18.6 us
  transfers between devices with their start and end apart: 3, of which 3 were waited for; matrix products, arithmetic and copies ran while one was open for 0% of the time, Pallas kernels for 0%

profile of v1, /device:TPU:0, one launch (start us, length us, event | category | flops | bytes accessed | tf_op | source)
XLA Modules:
  0.0 473.0 jit_solution(5241089670545290282)
XLA Ops:
  6.5 2.1 convert_element_type.20
  8.7 77.8 %all-gather.4.cloned.1.call-done = bf16[16384,256]{1,0:T(8,128)(2,1)} async-done(((bf16[1024,256]{1,0:T(8,128)(2,1)}), bf16[16384,256]{1,0:T(8,128)(2,1)}) %all-gather.4.cloned.1.call-update) | async-done | bytes 8388624 | tf_op jit(solution)/shard_map/all_gather | solution.py:20
  86.5 2.4 dynamic-slice_select_fusion
  89.0 0.7 convert_element_type.21
  89.7 31.1 %all-gather.6.cloned.1.call-done = bf16[4096,256]{1,0:T(8,128)(2,1)} async-done(((bf16[2048,256]{1,0:T(8,128)(2,1)}), bf16[4096,256]{1,0:T(8,128)(2,1)}) %all-gather.6.cloned.1.call-update) | async-done | bytes 2097168 | tf_op jit(solution)/shard_map/all_gather | solution.py:7
  120.8 2.6 reduce_sum.12
  123.4 165.5 %while.13 = (s32[]{:T(128)}, f32[32,512,256]{2,1,0:T(8,128)}, s32[32]{0:T(128)S(1)}, bf16[16384,256]{1,0:T(8,128)(2,1)}, bf16[2048,256]{1,0:T(8,128)(2,1)S(1)}, ...) while((s32[]{:T(128)}, f32[32,512,256]{2,1,0:T(8,128)}, ...), condition=%wide.region_2.3_spmd.clone, body=%wide.region_1.2_spmd.clone.sunk | while | flops 1080166912 | bytes 5011147 | solution.py:44
  123.4 0.6 dynamic_slice.35
  124.7 3.9 fusion.18
  129.9 3.9 fusion.18
  135.0 3.9 fusion.18
  140.2 3.9 fusion.18
  145.4 3.9 fusion.18
  150.5 3.9 fusion.18
  154.4 0.6 dynamic_slice.35
  155.7 3.9 fusion.18
  160.9 3.9 fusion.18
  166.0 3.9 fusion.18
  171.2 3.9 fusion.18
  175.1 0.6 dynamic_slice.35
  176.4 3.9 fusion.18
  181.6 3.9 fusion.18
  186.7 3.9 fusion.18
  191.9 3.9 fusion.18
  195.8 0.6 dynamic_slice.35
  197.1 3.9 fusion.18
  202.2 3.9 fusion.18
  207.4 3.9 fusion.18
  212.6 3.9 fusion.18
  216.6 0.6 dynamic_slice.35
  217.8 3.9 fusion.18
  223.0 3.9 fusion.18
  228.1 3.9 fusion.18
  232.0 0.6 dynamic_slice.35
  233.3 3.9 fusion.18
  237.2 0.6 dynamic_slice.35
  238.5 3.9 fusion.18
  242.4 0.6 dynamic_slice.35
  243.6 3.9 fusion.18
  248.8 3.9 fusion.18
  254.0 3.9 fusion.18
  259.2 3.9 fusion.18
  264.3 3.9 fusion.18
  269.5 3.9 fusion.18
  274.7 3.9 fusion.18
  279.8 3.9 fusion.18
  285.0 3.9 fusion.18
  288.9 177.5 %reduce-scatter.2.cloned.1.call-done = f32[1024,256]{1,0:T(8,128)} async-done(((f32[16384,256]{1,0:T(8,128)}), f32[1024,256]{1,0:T(8,128)}) %reduce-scatter.2.cloned.1.call-update) | async-done | bytes 1048592 | tf_op jit(solution)/shard_map/reduce_scatter | solution.py:45
  (96 shorter events, 14.5 us)
Async XLA Ops:
  6.5 80.0 %all-gather.4.cloned.1.call-start = ((), (), s32[]{:S(2)}) async-start(), calls=%async_computation.1 | async-start | bytes 8912896 | tf_op jit(solution)/shard_map/all_gather | solution.py:20
  8.6 112.1 %all-gather.6.cloned.1.call-start = ((), (), s32[]{:S(2)}) async-start(), calls=%async_computation.3 | async-start | bytes 3145728 | tf_op jit(solution)/shard_map/all_gather | solution.py:7
  88.9 377.5 %reduce-scatter.2.cloned.1.call-start = ((), (), s32[]{:S(2)}) async-start(), calls=%async_computation.2 | async-start | bytes 17825792 | tf_op jit(solution)/shard_map/reduce_scatter | solution.py:45
Sparse Core Ops, SparseCore 0:
  9.5 77.0 all-gather.3
  89.1 31.6 all-gather.5
  289.1 177.3 reduce-scatter.1
